TPU v7x, 32 devices: a whole 2x2x4 slice. The times are simulated.
32 devices in a mesh: groups: 2 (over y), batch: 4 (over z), blk: 4 (over x, core).
Axes of the slice: x: 2, y: 2, z: 4, core: 2. Of those that a mesh axis runs over, the one named last changes fastest.
Arguments:
- queries: bfloat16 [8, 592, 1024], P(('groups', 'batch'), 'blk'), parts along dimension 0, may hold values from -12 to 12
- key_states: bfloat16 [8, 592, 1024], P(('groups', 'batch'), 'blk'), parts along dimension 0, may hold values from -6 to 6
- value_states: bfloat16 [8, 592, 1024], P(('groups', 'batch'), 'blk'), parts along dimension 0, may hold values from -6 to 6
- residual: bfloat16 [8, 592, 768], P(('groups', 'batch'), 'blk'), parts along dimension 0, may hold values from -3 to 3
- proj_weight: bfloat16 [1024, 768], P(None, 'batch'), may hold values from -0.1875 to 0.1875
- conv_weight: bfloat16 [3, 3, 768, 384], P(None, None, 'batch'), may hold values from -0.078125 to 0.078125
Outputs:
- conv_out: bfloat16 [8, 592, 384], P(('groups', 'batch'), 'blk'), parts along dimension 0
There are 2 independent parts, one for each index of `groups`. A program takes and returns all parts, laid end to end along the dimension named above; an argument that names none is the same for every part. Nothing has to cross between parts.
All inputs are finite; a program needn't handle non-finite values.
Results may differ from a plain program's by a relative error of at most 0.0085.
Values may be sent and summed in bfloat16 or wider, within the bound.
A program may use at most 64 MiB of HBM per device.

v0:
```python
import jax
import jax.numpy as jnp
from jax import lax
from jax.sharding import PartitionSpec as P

HEADS = 16
HD = 64
COLS = 74
ROWS = 2


def extended(cells, sides, width):
    for axis, dim in sides:
        count = lax.axis_size(axis)
        ends = count - 1
        head = lax.slice_in_dim(cells, 0, width, axis=dim)
        tail = lax.slice_in_dim(cells, cells.shape[dim] - width, cells.shape[dim], axis=dim)
        cells = jnp.concatenate(
            [
                lax.ppermute(tail, axis, [(i, (i + 1) % count) for i in range(ends)]),
                cells,
                lax.ppermute(head, axis, [((i + 1) % count, i) for i in range(ends)]),
            ],
            axis=dim,
        )
    return cells


def empty_state(head_count, query_rows):
    return (
        jnp.full((head_count, query_rows), -1e30, jnp.float32),
        jnp.zeros((head_count, query_rows), jnp.float32),
        jnp.zeros((head_count, query_rows, HD), jnp.float32),
    )


def absorb(carry_state, query_block, key_block, value_block):
    row_max, weight_sum, running = carry_state
    scores = jnp.einsum(
        "qhd,khd->hqk", query_block, key_block, preferred_element_type=jnp.float32
    ) * HD ** (-0.5)
    new_max = jnp.maximum(row_max, jnp.max(scores, axis=2))
    factor = jnp.exp(row_max - new_max)
    weights = jnp.exp(scores - new_max[:, :, None])
    weight_sum = weight_sum * factor + jnp.sum(weights, axis=2)
    running = running * factor[:, :, None] + jnp.einsum(
        "hqk,khd->hqd",
        weights.astype(jnp.bfloat16),
        value_block,
        preferred_element_type=jnp.float32,
    )
    return (new_max, weight_sum, running)


def finish(carry_state):
    row_max, weight_sum, running = carry_state
    mixed = running / weight_sum[:, :, None]
    head_count, query_rows = weight_sum.shape
    return mixed.transpose(1, 0, 2).reshape(query_rows, head_count * HD).astype(jnp.bfloat16)


def body(queries, key_states, value_states, residual, proj_weight, conv_weight):
    query_rows = queries[0]
    key_rows = key_states[0]
    value_rows = value_states[0]
    tok_rows = query_rows.shape[0]
    cycle_count = lax.axis_size("blk")
    local_heads = HEADS // cycle_count
    query_all, key_all, value_all = (
        lax.all_to_all(query_rows, "blk", split_axis=1, concat_axis=0, tiled=True),
        lax.all_to_all(key_rows, "blk", split_axis=1, concat_axis=0, tiled=True),
        lax.all_to_all(value_rows, "blk", split_axis=1, concat_axis=0, tiled=True),
    )
    seq_rows = tok_rows * cycle_count
    group = 1
    while cycle_count % (group * 2) == 0 and tok_rows * group * 2 <= 1024:
        group = group * 2
    block_rows = tok_rows * group
    block_count = seq_rows // block_rows
    query_blocks = query_all.reshape(block_count, block_rows, local_heads, HD)
    key_blocks = key_all.reshape(block_count, block_rows, local_heads, HD)
    value_blocks = value_all.reshape(block_count, block_rows, local_heads, HD)

    def one_block(query_block):

        def absorb_one(index, inner_state):
            return absorb(inner_state, query_block, key_blocks[index], value_blocks[index])

        return finish(
            lax.fori_loop(0, block_count, absorb_one, empty_state(local_heads, block_rows))
        )

    mixed_rows = lax.map(one_block, query_blocks).reshape(seq_rows, local_heads * HD)
    attention = lax.all_to_all(mixed_rows, "blk", split_axis=0, concat_axis=1, tiled=True)
    projected = jnp.dot(
        attention,
        lax.all_gather(proj_weight, "batch", axis=1, tiled=True),
        preferred_element_type=jnp.float32,
    )
    hidden = (residual[0].astype(jnp.float32) + projected).astype(jnp.bfloat16)
    feature_grid = hidden.reshape(ROWS, COLS, hidden.shape[1])
    rimmed = extended(feature_grid, (("blk", 0),), 1)
    padded = jnp.pad(rimmed, ((0, 0), (1, 1), (0, 0)))
    shard_piece = lax.all_gather(conv_weight, "batch", axis=2, tiled=True)
    piece_rows = shard_piece.shape[2]
    windows = []
    for row_off in range(3):
        for col_off in range(3):
            windows.append(
                padded[row_off : row_off + ROWS, col_off : col_off + COLS].reshape(
                    tok_rows, piece_rows
                )
            )
    stacked = jnp.concatenate(windows, axis=1)
    flat_weight = shard_piece.reshape(9 * piece_rows, shard_piece.shape[3])
    conv_sum = jnp.dot(stacked, flat_weight, preferred_element_type=jnp.float32)
    return conv_sum.astype(jnp.bfloat16)[None]


def solution(mesh):
    return jax.shard_map(
        body,
        mesh=mesh,
        in_specs=(
            P(("groups", "batch"), "blk", None),
            P(("groups", "batch"), "blk", None),
            P(("groups", "batch"), "blk", None),
            P(("groups", "batch"), "blk", None),
            P(None, "batch"),
            P(None, None, "batch", None),
        ),
        out_specs=P(("groups", "batch"), "blk", None),
        check_vma=False,
    )
```

profile of v0, /device:TPU:0, one launch (start us, length us, event | category | flops | bytes accessed | tf_op | source)
XLA Modules:
  0.0 159.6 jit_solution(15283503268794246920)
XLA Ops:
  8.0 1.2 all_to_all.48
  9.9 4.2 %all-to-all-start = ((bf16[148,4,256]{2,0,1:T(8,128)(2,1)}), bf16[148,4,256]{2,0,1:T(8,128)(2,1)S(1)}, u32[]{:S(2)}, u32[]{:S(2)}) async-start(bf16[148,4,256]{2,0,1:T(8,128)(2,1)} %copy.22), calls=%async_computation | async-start | bytes 622592 | tf_op jit(solution)/shard_map/all_to_all | solution.py:70
  14.3 0.8 copy.24
  15.1 5.6 %all-to-all-done = bf16[148,4,256]{2,0,1:T(8,128)(2,1)S(1)} async-done(((bf16[148,4,256]{2,0,1:T(8,128)(2,1)}), bf16[148,4,256]{2,0,1:T(8,128)(2,1)S(1)}, u32[]{:S(2)}, u32[]{:S(2)}) %all-to-all-start) | async-done | bytes 303136 | tf_op jit(solution)/shard_map/all_to_all | solution.py:70
  20.7 3.5 %all-to-all-start.1 = ((bf16[148,4,256]{2,0,1:T(8,128)(2,1)}), bf16[148,4,256]{2,0,1:T(8,128)(2,1)S(1)}, u32[]{:S(2)}, u32[]{:S(2)}) async-start(bf16[148,4,256]{2,0,1:T(8,128)(2,1)} %copy.24), calls=%async_computation.1 | async-start | bytes 622592 | tf_op jit(solution)/shard_map/all_to_all | solution.py:71
  25.0 5.6 %all-to-all-done.1 = bf16[148,4,256]{2,0,1:T(8,128)(2,1)S(1)} async-done(((bf16[148,4,256]{2,0,1:T(8,128)(2,1)}), bf16[148,4,256]{2,0,1:T(8,128)(2,1)S(1)}, u32[]{:S(2)}, u32[]{:S(2)}) %all-to-all-start.1) | async-done | bytes 303136 | tf_op jit(solution)/shard_map/all_to_all | solution.py:71
  30.6 3.5 %all-to-all-start.2 = ((bf16[148,4,256]{2,0,1:T(8,128)(2,1)}), bf16[148,4,256]{2,0,1:T(8,128)(2,1)S(1)}, u32[]{:S(2)}, u32[]{:S(2)}) async-start(bf16[148,4,256]{2,0,1:T(8,128)(2,1)} %copy.26), calls=%async_computation.2 | async-start | bytes 622592 | tf_op jit(solution)/shard_map/all_to_all | solution.py:72
  34.7 5.9 %all-to-all-done.2 = bf16[148,4,256]{2,0,1:T(8,128)(2,1)S(1)} async-done(((bf16[148,4,256]{2,0,1:T(8,128)(2,1)}), bf16[148,4,256]{2,0,1:T(8,128)(2,1)S(1)}, u32[]{:S(2)}, u32[]{:S(2)}) %all-to-all-start.2) | async-done | bytes 303136 | tf_op jit(solution)/shard_map/all_to_all | solution.py:72
  40.9 1.1 multiply_reduce_fusion
  42.0 1.0 fusion
  43.1 1.3 fusion.17
  45.1 8.9 %all_to_all.64 = bf16[4,148,256]{2,1,0:T(8,128)(2,1)S(1)} all-to-all(bf16[4,148,256]{2,1,0:T(8,128)(2,1)S(1)} %copy.29), channel_id=1, replica_groups=mesh['groups'=2,'batch'=4,'blk'=4] {'blk'}, dimensions={0} | all-to-all | bytes 606208 | tf_op jit(solution)/shard_map/all_to_all | solution.py:94
  54.3 2.2 %fusion.12 = bf16[148,768]{1,0:T(8,128)(2,1)S(1)} fusion(bf16[148,1024]{1,0:T(8,128)(2,1)S(1)} %bitcast.41, bf16[1024,768]{0,1:T(8,128)(2,1)} %all-gather.3.cloned.1.call-done, bf16[1,148,768]{2,1,0:T(8,128)(2,1)S(1)} %copy-done.2), kind=kOutput, calls=%fused_computation.12 | convolution fusion | flops 233124864 | bytes 2330624 | tf_op jit(solution)/shard_map/dot_general | solution.py:95
  56.5 1.7 %collective-permute-start = (bf16[1,74,768]{2,1,0:T(8,128)(2,1)S(1)}, bf16[1,74,768]{2,1,0:T(8,128)(2,1)S(1)}, u32[]{:S(2)}, u32[]{:S(2)}) collective-permute-start(bf16[1,74,768]{2,1,0:T(8,128)(2,1)S(1)} %get-tuple-element.60), channel_id=1, source_target_pairs={{0,1},{1,2},{2,3},{4,5},{5,6},{6,7},{8,9},{9,10},{10,11},{12,13},{... | collective-permute-start | bytes 341000 | tf_op jit(solution)/shard_map/ppermute | solution.py:20
  58.2 1.3 collective-permute-start.1
  59.6 2.0 %collective-permute-done.1 = bf16[1,74,768]{2,1,0:T(8,128)(2,1)S(1)} collective-permute-done((bf16[1,74,768]{2,1,0:T(8,128)(2,1)S(1)}, bf16[1,74,768]{2,1,0:T(8,128)(2,1)S(1)}, u32[]{:S(2)}, u32[]{:S(2)}) %collective-permute-start.1) | collective-permute-done | bytes 113696 | tf_op jit(solution)/shard_map/ppermute | solution.py:22
  62.0 0.8 reshape.82
  62.8 0.8 reshape.83
  63.5 0.8 reshape.84
  64.5 1.0 constant_dynamic-update-slice_fusion.7
  65.5 1.0 constant_dynamic-update-slice_fusion.6
  66.5 1.0 constant_dynamic-update-slice_fusion.5
  67.5 80.7 %all-gather.5.cloned.1.call-done = bf16[3,3,768,384]{3,2,1,0:T(8,128)(2,1)} async-done(((bf16[3,3,192,384]{3,2,1,0:T(8,128)(2,1)}), bf16[3,3,768,384]{3,2,1,0:T(8,128)(2,1)}) %all-gather.5.cloned.1.call-update) | async-done | bytes 5308432 | tf_op jit(solution)/shard_map/all_gather | solution.py:104
  148.3 4.5 %fusion.13 = bf16[1,148,384]{2,1,0:T(8,128)(2,1)} fusion(bf16[148,6912]{1,0:T(8,128)(2,1)S(1)} %constant_dynamic-update-slice_fusion, bf16[6912,384]{1,0:T(8,128)(2,1)} %bitcast.37), kind=kOutput, calls=%fused_computation.14 | convolution fusion | flops 785702400 | bytes 7468032 | tf_op jit(solution)/shard_map/dot_general | solution.py:116
  (42 shorter events, 5.8 us)
Async XLA Ops:
  6.5 7.6 %copy-start = (bf16[1,148,1024]{2,1,0:T(8,128)(2,1)S(1)}, bf16[1,148,1024]{2,1,0:T(8,128)(2,1)}, u32[]{:S(2)}) copy-start(bf16[1,148,1024]{2,1,0:T(8,128)(2,1)} %param.7) | copy-start | bytes 909316
  6.5 47.8 %all-gather.3.cloned.1.call-start = ((), (), s32[]{:S(2)}) async-start(), calls=%async_computation.4 | async-start | bytes 1966080 | tf_op jit(solution)/shard_map/all_gather | solution.py:97
  7.3 141.0 %all-gather.5.cloned.1.call-start = ((), (), s32[]{:S(2)}) async-start(), calls=%async_computation.5 | async-start | bytes 6635520 | tf_op jit(solution)/shard_map/all_gather | solution.py:104
  8.0 16.1 %copy-start.1 = (bf16[1,148,1024]{2,1,0:T(8,128)(2,1)S(1)}, bf16[1,148,1024]{2,1,0:T(8,128)(2,1)}, u32[]{:S(2)}) copy-start(bf16[1,148,1024]{2,1,0:T(8,128)(2,1)} %param.8) | copy-start | bytes 909316
  9.9 10.8 %all-to-all-start = ((bf16[148,4,256]{2,0,1:T(8,128)(2,1)}), bf16[148,4,256]{2,0,1:T(8,128)(2,1)S(1)}, u32[]{:S(2)}, u32[]{:S(2)}) async-start(bf16[148,4,256]{2,0,1:T(8,128)(2,1)} %copy.22), calls=%async_computation | async-start | bytes 622592 | tf_op jit(solution)/shard_map/all_to_all | solution.py:70
  20.7 10.0 %all-to-all-start.1 = ((bf16[148,4,256]{2,0,1:T(8,128)(2,1)}), bf16[148,4,256]{2,0,1:T(8,128)(2,1)S(1)}, u32[]{:S(2)}, u32[]{:S(2)}) async-start(bf16[148,4,256]{2,0,1:T(8,128)(2,1)} %copy.24), calls=%async_computation.1 | async-start | bytes 622592 | tf_op jit(solution)/shard_map/all_to_all | solution.py:71
  30.6 10.0 %all-to-all-start.2 = ((bf16[148,4,256]{2,0,1:T(8,128)(2,1)}), bf16[148,4,256]{2,0,1:T(8,128)(2,1)S(1)}, u32[]{:S(2)}, u32[]{:S(2)}) async-start(bf16[148,4,256]{2,0,1:T(8,128)(2,1)} %copy.26), calls=%async_computation.2 | async-start | bytes 622592 | tf_op jit(solution)/shard_map/all_to_all | solution.py:72
  44.4 9.9 %copy-start.2 = (bf16[1,148,768]{2,1,0:T(8,128)(2,1)S(1)}, bf16[1,148,768]{2,1,0:T(8,128)(2,1)}, u32[]{:S(2)}) copy-start(bf16[1,148,768]{2,1,0:T(8,128)(2,1)} %param.9) | copy-start | bytes 681988
  56.5 3.0 %collective-permute-start = (bf16[1,74,768]{2,1,0:T(8,128)(2,1)S(1)}, bf16[1,74,768]{2,1,0:T(8,128)(2,1)S(1)}, u32[]{:S(2)}, u32[]{:S(2)}) collective-permute-start(bf16[1,74,768]{2,1,0:T(8,128)(2,1)S(1)} %get-tuple-element.60), channel_id=1, source_target_pairs={{0,1},{1,2},{2,3},{4,5},{5,6},{6,7},{8,9},{9,10},{10,11},{12,13},{... | collective-permute-start | bytes 341000 | tf_op jit(solution)/shard_map/ppermute | solution.py:20
  58.2 3.4 %collective-permute-start.1 = (bf16[1,74,768]{2,1,0:T(8,128)(2,1)S(1)}, bf16[1,74,768]{2,1,0:T(8,128)(2,1)S(1)}, u32[]{:S(2)}, u32[]{:S(2)}) collective-permute-start(bf16[1,74,768]{2,1,0:T(8,128)(2,1)S(1)} %get-tuple-element.61), channel_id=1, source_target_pairs={{1,0},{2,1},{3,2},{5,4},{6,5},{7,6},{9,8},{10,9},{11,10},{13,12},{... | collective-permute-start | bytes 341000 | tf_op jit(solution)/shard_map/ppermute | solution.py:22
Sparse Core Ops, SparseCore 0:
  8.9 39.7 all-gather.2
  50.2 97.9 all-gather.4
where the time goes:
time: 160 us
  waiting for transfers between devices  101 us (63%)
  starting transfers between devices  14.1 us (9%)
  between operations  13.7 us (9%)
  local copies, waits for them, and re-layouts  11.2 us (7%)
  matrix products  9.04 us (6%)
  blocking collectives  8.9 us (6%)
    all_gather x1, waiting for transfers between devices, body(): shard_piece = lax.all_gather(conv_weight, 'batch', axis=2, tiled=True)  80.7 us
    all_to_all x1, blocking collectives, body(): lax.all_to_all(mixed_rows, 'blk', split_axis=0, concat_axis=1, tiled=True)  8.9 us
    all_to_all x1, waiting for transfers between devices, body(): lax.all_to_all(value_rows, 'blk', split_axis=1, concat_axis=0, tiled=True)  5.92 us
    all_to_all x1, waiting for transfers between devices, body(): lax.all_to_all(query_rows, 'blk', split_axis=1, concat_axis=0, tiled=True)  5.62 us
    all_to_all x1, waiting for transfers between devices, body(): lax.all_to_all(key_rows, 'blk', split_axis=1, concat_axis=0, tiled=True)  5.6 us
    dot_general x1, matrix products, body(): conv_sum = jnp.dot(stacked, flat_weight, preferred_element_type=jnp.float32)  4.48 us
    all_to_all x1, starting transfers between devices, body(): lax.all_to_all(query_rows, 'blk', split_axis=1, concat_axis=0, tiled=True)  4.24 us
    all_to_all x1, starting transfers between devices, body(): lax.all_to_all(value_rows, 'blk', split_axis=1, concat_axis=0, tiled=True)  3.45 us
  transfers between devices with their start and end apart: 7, of which 5 were waited for; matrix products, arithmetic and copies ran while one was open for 10% of the time, Pallas kernels for 0%

commit v1 on v0

--- a/solution.py
+++ b/solution.py
@@ -68,7 +68,12 @@
     local_heads = HEADS // cycle_count
     query_all, key_all, value_all = (
         lax.all_to_all(query_rows, "blk", split_axis=1, concat_axis=0, tiled=True),
-        lax.all_to_all(key_rows, "blk", split_axis=1, concat_axis=0, tiled=True),
+        jnp.concatenate(
+            lax.all_to_all(
+                jnp.stack(jnp.split(key_rows, lax.axis_size("blk"), axis=1)), "blk", 0, 0
+            ),
+            axis=0,
+        ),
         lax.all_to_all(value_rows, "blk", split_axis=1, concat_axis=0, tiled=True),
     )
     seq_rows = tok_rows * cycle_count

time: 160 us -> 160 us (level)
  no operation moved by 1% of the time
where the time goes in v1:
time: 160 us
  waiting for transfers between devices  102 us (64%)
  starting transfers between devices  14.2 us (9%)
  between operations  13.7 us (9%)
  local copies, waits for them, and re-layouts  10.3 us (6%)
  blocking collectives  8.9 us (6%)
  matrix products  8.85 us (6%)
  other arithmetic  2.02 us (1%)
    all_gather x1, waiting for transfers between devices, body(): shard_piece = lax.all_gather(conv_weight, 'batch', axis=2, tiled=True)  80.9 us
    all_to_all x1, blocking collectives, body(): lax.all_to_all(mixed_rows, 'blk', split_axis=0, concat_axis=1, tiled=True)  8.9 us
    all_to_all x1, waiting for transfers between devices, body(): lax.all_to_all(jnp.stack(jnp.split(key_rows, lax.axis_size('blk'), axis=1...  5.92 us
    all_to_all x1, waiting for transfers between devices, body(): lax.all_to_all(value_rows, 'blk', split_axis=1, concat_axis=0, tiled=True)  5.71 us
    all_to_all x1, waiting for transfers between devices, body(): lax.all_to_all(query_rows, 'blk', split_axis=1, concat_axis=0, tiled=True)  5.61 us
    dot_general x1, matrix products, body(): conv_sum = jnp.dot(stacked, flat_weight, preferred_element_type=jnp.float32)  4.48 us
    all_to_all x1, starting transfers between devices, body(): lax.all_to_all(query_rows, 'blk', split_axis=1, concat_axis=0, tiled=True)  4.24 us
    all_to_all x1, starting transfers between devices, body(): lax.all_to_all(jnp.stack(jnp.split(key_rows, lax.axis_size('blk'), axis=1...  3.45 us
  transfers between devices with their start and end apart: 7, of which 5 were waited for; matrix products, arithmetic and copies ran while one was open for 10% of the time, Pallas kernels for 0%

profile of v1, /device:TPU:0, one launch (start us, length us, event | category | flops | bytes accessed | tf_op | source)
XLA Modules:
  0.0 159.6 jit_solution(10032020959119484924)
XLA Ops:
  8.0 1.2 all_to_all.40
  9.9 4.2 %all-to-all-start.1 = ((bf16[148,4,256]{2,0,1:T(8,128)(2,1)}), bf16[148,4,256]{2,0,1:T(8,128)(2,1)S(1)}, u32[]{:S(2)}, u32[]{:S(2)}) async-start(bf16[148,4,256]{2,0,1:T(8,128)(2,1)} %copy.23), calls=%async_computation.1 | async-start | bytes 622592 | tf_op jit(solution)/shard_map/all_to_all | solution.py:70
  14.3 0.8 copy.25
  15.1 5.6 %all-to-all-done.1 = bf16[148,4,256]{2,0,1:T(8,128)(2,1)S(1)} async-done(((bf16[148,4,256]{2,0,1:T(8,128)(2,1)}), bf16[148,4,256]{2,0,1:T(8,128)(2,1)S(1)}, u32[]{:S(2)}, u32[]{:S(2)}) %all-to-all-start.1) | async-done | bytes 303136 | tf_op jit(solution)/shard_map/all_to_all | solution.py:70
  20.7 3.5 %all-to-all-start.2 = ((bf16[148,4,256]{2,0,1:T(8,128)(2,1)}), bf16[148,4,256]{2,0,1:T(8,128)(2,1)S(1)}, u32[]{:S(2)}, u32[]{:S(2)}) async-start(bf16[148,4,256]{2,0,1:T(8,128)(2,1)} %copy.25), calls=%async_computation.2 | async-start | bytes 622592 | tf_op jit(solution)/shard_map/all_to_all | solution.py:77
  24.2 0.8 pad_maximum_fusion
  24.9 5.7 %all-to-all-done.2 = bf16[148,4,256]{2,0,1:T(8,128)(2,1)S(1)} async-done(((bf16[148,4,256]{2,0,1:T(8,128)(2,1)}), bf16[148,4,256]{2,0,1:T(8,128)(2,1)S(1)}, u32[]{:S(2)}, u32[]{:S(2)}) %all-to-all-start.2) | async-done | bytes 303136 | tf_op jit(solution)/shard_map/all_to_all | solution.py:77
  30.6 3.5 %all-to-all-start = ((bf16[4,148,256]{2,1,0:T(8,128)(2,1)}), bf16[4,148,256]{2,1,0:T(8,128)(2,1)S(1)}, u32[]{:S(2)}, u32[]{:S(2)}) async-start(bf16[4,148,256]{2,1,0:T(8,128)(2,1)} %pad_maximum_fusion), calls=%async_computation | async-start | bytes 622592 | tf_op jit(solution)/shard_map/all_to_all | solution.py:72
  34.7 5.9 %all-to-all-done = bf16[4,148,256]{2,1,0:T(8,128)(2,1)S(1)} async-done(((bf16[4,148,256]{2,1,0:T(8,128)(2,1)}), bf16[4,148,256]{2,1,0:T(8,128)(2,1)S(1)}, u32[]{:S(2)}, u32[]{:S(2)}) %all-to-all-start) | async-done | bytes 303136 | tf_op jit(solution)/shard_map/all_to_all | solution.py:72
  40.9 1.0 bitcast_reduce_fusion
  41.9 1.0 fusion.1
  43.0 1.3 fusion.18
  44.9 8.9 %all_to_all.53 = bf16[4,148,256]{2,1,0:T(8,128)(2,1)S(1)} all-to-all(bf16[4,148,256]{2,1,0:T(8,128)(2,1)S(1)} %copy.28), channel_id=1, replica_groups=mesh['groups'=2,'batch'=4,'blk'=4] {'blk'}, dimensions={0} | all-to-all | bytes 606208 | tf_op jit(solution)/shard_map/all_to_all | solution.py:99
  54.2 2.1 %fusion.13 = bf16[148,768]{1,0:T(8,128)(2,1)S(1)} fusion(bf16[148,1024]{1,0:T(8,128)(2,1)S(1)} %bitcast.66, bf16[1024,768]{0,1:T(8,128)(2,1)} %all-gather.3.cloned.1.call-done, bf16[1,148,768]{2,1,0:T(8,128)(2,1)S(1)} %copy-done.2), kind=kOutput, calls=%fused_computation.13 | convolution fusion | flops 233124864 | bytes 2330624 | tf_op jit(solution)/shard_map/dot_general | solution.py:100
  56.4 1.7 %collective-permute-start = (bf16[1,74,768]{2,1,0:T(8,128)(2,1)S(1)}, bf16[1,74,768]{2,1,0:T(8,128)(2,1)S(1)}, u32[]{:S(2)}, u32[]{:S(2)}) collective-permute-start(bf16[1,74,768]{2,1,0:T(8,128)(2,1)S(1)} %get-tuple-element.64), channel_id=1, source_target_pairs={{0,1},{1,2},{2,3},{4,5},{5,6},{6,7},{8,9},{9,10},{10,11},{12,13},{... | collective-permute-start | bytes 341000 | tf_op jit(solution)/shard_map/ppermute | solution.py:20
  58.1 1.3 collective-permute-start.1
  59.4 2.0 %collective-permute-done.1 = bf16[1,74,768]{2,1,0:T(8,128)(2,1)S(1)} collective-permute-done((bf16[1,74,768]{2,1,0:T(8,128)(2,1)S(1)}, bf16[1,74,768]{2,1,0:T(8,128)(2,1)S(1)}, u32[]{:S(2)}, u32[]{:S(2)}) %collective-permute-start.1) | collective-permute-done | bytes 113696 | tf_op jit(solution)/shard_map/ppermute | solution.py:22
  61.8 0.8 reshape.75
  62.6 0.7 reshape.77
  64.3 1.0 constant_dynamic-update-slice_fusion.8
  65.3 1.0 constant_dynamic-update-slice_fusion.6
  66.3 1.0 constant_dynamic-update-slice_fusion.5
  67.4 80.9 %all-gather.5.cloned.1.call-done = bf16[3,3,768,384]{3,2,1,0:T(8,128)(2,1)} async-done(((bf16[3,3,192,384]{3,2,1,0:T(8,128)(2,1)}), bf16[3,3,768,384]{3,2,1,0:T(8,128)(2,1)}) %all-gather.5.cloned.1.call-update) | async-done | bytes 5308432 | tf_op jit(solution)/shard_map/all_gather | solution.py:109
  148.3 4.5 %fusion.14 = bf16[1,148,384]{2,1,0:T(8,128)(2,1)} fusion(bf16[148,6912]{1,0:T(8,128)(2,1)S(1)} %constant_dynamic-update-slice_fusion, bf16[6912,384]{1,0:T(8,128)(2,1)} %bitcast.63), kind=kOutput, calls=%fused_computation.15 | convolution fusion | flops 785702400 | bytes 7468032 | tf_op jit(solution)/shard_map/dot_general | solution.py:121
  (42 shorter events, 5.7 us)
Async XLA Ops:
  6.5 7.6 %copy-start = (bf16[1,148,1024]{2,1,0:T(8,128)(2,1)S(1)}, bf16[1,148,1024]{2,1,0:T(8,128)(2,1)}, u32[]{:S(2)}) copy-start(bf16[1,148,1024]{2,1,0:T(8,128)(2,1)} %param.8) | copy-start | bytes 909316
  6.5 47.6 %all-gather.3.cloned.1.call-start = ((), (), s32[]{:S(2)}) async-start(), calls=%async_computation.4 | async-start | bytes 1966080 | tf_op jit(solution)/shard_map/all_gather | solution.py:102
  7.3 141.0 %all-gather.5.cloned.1.call-start = ((), (), s32[]{:S(2)}) async-start(), calls=%async_computation.5 | async-start | bytes 6635520 | tf_op jit(solution)/shard_map/all_gather | solution.py:109
  8.0 16.1 %copy-start.1 = (bf16[1,148,1024]{2,1,0:T(8,128)(2,1)S(1)}, bf16[1,148,1024]{2,1,0:T(8,128)(2,1)}, u32[]{:S(2)}) copy-start(bf16[1,148,1024]{2,1,0:T(8,128)(2,1)} %param.7) | copy-start | bytes 909316
  9.9 10.8 %all-to-all-start.1 = ((bf16[148,4,256]{2,0,1:T(8,128)(2,1)}), bf16[148,4,256]{2,0,1:T(8,128)(2,1)S(1)}, u32[]{:S(2)}, u32[]{:S(2)}) async-start(bf16[148,4,256]{2,0,1:T(8,128)(2,1)} %copy.23), calls=%async_computation.1 | async-start | bytes 622592 | tf_op jit(solution)/shard_map/all_to_all | solution.py:70
  20.7 10.0 %all-to-all-start.2 = ((bf16[148,4,256]{2,0,1:T(8,128)(2,1)}), bf16[148,4,256]{2,0,1:T(8,128)(2,1)S(1)}, u32[]{:S(2)}, u32[]{:S(2)}) async-start(bf16[148,4,256]{2,0,1:T(8,128)(2,1)} %copy.25), calls=%async_computation.2 | async-start | bytes 622592 | tf_op jit(solution)/shard_map/all_to_all | solution.py:77
  30.6 10.0 %all-to-all-start = ((bf16[4,148,256]{2,1,0:T(8,128)(2,1)}), bf16[4,148,256]{2,1,0:T(8,128)(2,1)S(1)}, u32[]{:S(2)}, u32[]{:S(2)}) async-start(bf16[4,148,256]{2,1,0:T(8,128)(2,1)} %pad_maximum_fusion), calls=%async_computation | async-start | bytes 622592 | tf_op jit(solution)/shard_map/all_to_all | solution.py:72
  44.2 9.9 %copy-start.2 = (bf16[1,148,768]{2,1,0:T(8,128)(2,1)S(1)}, bf16[1,148,768]{2,1,0:T(8,128)(2,1)}, u32[]{:S(2)}) copy-start(bf16[1,148,768]{2,1,0:T(8,128)(2,1)} %param.9) | copy-start | bytes 681988
  56.4 3.1 %collective-permute-start = (bf16[1,74,768]{2,1,0:T(8,128)(2,1)S(1)}, bf16[1,74,768]{2,1,0:T(8,128)(2,1)S(1)}, u32[]{:S(2)}, u32[]{:S(2)}) collective-permute-start(bf16[1,74,768]{2,1,0:T(8,128)(2,1)S(1)} %get-tuple-element.64), channel_id=1, source_target_pairs={{0,1},{1,2},{2,3},{4,5},{5,6},{6,7},{8,9},{9,10},{10,11},{12,13},{... | collective-permute-start | bytes 341000 | tf_op jit(solution)/shard_map/ppermute | solution.py:20
  58.1 3.4 %collective-permute-start.1 = (bf16[1,74,768]{2,1,0:T(8,128)(2,1)S(1)}, bf16[1,74,768]{2,1,0:T(8,128)(2,1)S(1)}, u32[]{:S(2)}, u32[]{:S(2)}) collective-permute-start(bf16[1,74,768]{2,1,0:T(8,128)(2,1)S(1)} %get-tuple-element.65), channel_id=1, source_target_pairs={{1,0},{2,1},{3,2},{5,4},{6,5},{7,6},{9,8},{10,9},{11,10},{13,12},{... | collective-permute-start | bytes 341000 | tf_op jit(solution)/shard_map/ppermute | solution.py:22
Sparse Core Ops, SparseCore 0:
  8.9 39.7 all-gather.2
  50.2 97.9 all-gather.4
